TPU v7x, 32 devices: a whole 2x2x4 slice. The times are simulated.
32 devices in a mesh: row: 4 (over x, core), col: 8 (over z, y).
Axes of the slice: x: 2, y: 2, z: 4, core: 2. Of those that a mesh axis runs over, the one named last changes fastest.
Arguments:
- momentum: bfloat16 [8704, 30720], P('row', 'col'), may hold values from -6 to 6
- grad: bfloat16 [8704, 30720], P('row', 'col'), may hold values from -6 to 6
- q_prev: bfloat16 [30720, 512], P('col'), may hold values from -6 to 6
- row_counts: int32 [4], replicated, may hold values from 1 to 17, 64 in all
- col_counts: int32 [8], replicated, may hold values from 1 to 30, 224 in all
Outputs:
- momentum_out: bfloat16 [8704, 30720], P('row', 'col')
- basis_out: bfloat16 [30720, 512], P('col')
- update: bfloat16 [8704, 30720], P('row', 'col')
Inputs may be any that keep to these rules, and one draw needn't show every extreme that they name: `row_counts`: each index of row holds 1 to 17 live row blocks, the counts sum to 64, and some index holds exactly 17; live blocks are the first slots of a device. `col_counts`: each index of col holds 1 to 30 live column blocks, the counts sum to 224, and some index holds exactly 30; live blocks are the first slots of a device.
All inputs are finite; a program needn't handle non-finite values.
Results may differ from a plain program's by a relative error of at most 0.0079.
Values may be sent and summed in bfloat16 or wider, within the bound.
No kernel may reach another device: no remote copies, remote signals or barrier semaphores. Data moves between devices by JAX's collectives and lax.ppermute only.
A program may use at most 128 MiB of HBM per device.

v0:
```python
import math

import jax
import jax.numpy as jnp
from jax import lax
from jax.sharding import PartitionSpec as P

D = 8192
FF = 28672
RANK = 512
BLOCK = 128


EPS = 1e-06
ERR = 0.05


def tri_inverse(gram_matrix):
    lower_factor = jnp.linalg.cholesky(gram_matrix)
    ident = jnp.eye(gram_matrix.shape[0], dtype=gram_matrix.dtype)
    return jax.scipy.linalg.solve_triangular(lower_factor, ident, lower=True)


def on_device(momentum, grad, q_prev, row_counts, col_counts):
    row_slots, col_slots = momentum.shape
    row_live = row_counts[lax.axis_index("row")] * BLOCK
    col_live = col_counts[lax.axis_index("col")] * BLOCK
    row_mask = jnp.arange(row_slots, dtype=jnp.int32) < row_live
    col_mask = jnp.arange(col_slots, dtype=jnp.int32) < col_live
    summed = (momentum.astype(jnp.float32) + grad.astype(jnp.float32)).astype(jnp.bfloat16)
    buffer = jnp.where(row_mask[:, None] & col_mask[None, :], summed, jnp.zeros((), jnp.bfloat16))
    prev_basis = jnp.where(col_mask[:, None], q_prev, jnp.zeros((), jnp.bfloat16))
    partial_left = jnp.dot(buffer, prev_basis, preferred_element_type=jnp.float32)
    left_part = lax.psum(partial_left, "col")
    gram_local = jnp.dot(left_part.T, left_part, precision=lax.Precision.HIGHEST)
    gram_matrix = lax.psum(gram_local, "row")
    inverse = tri_inverse(gram_matrix)
    ortho = jnp.dot(left_part, inverse.T, precision=lax.Precision.HIGHEST).astype(jnp.bfloat16)
    right_part = lax.psum_scatter(
        lax.dot_general(
            buffer, ortho, (((0,), (0,)), ((), ())), preferred_element_type=jnp.float32
        ),
        "row",
        scatter_dimension=0,
        tiled=True,
    )
    squares = lax.psum(jnp.sum(right_part * right_part, axis=0), ("row", "col"))
    norm_factor = lax.rsqrt(squares / FF + EPS)
    right_piece = right_part.astype(jnp.bfloat16)
    basis_piece = (right_part * norm_factor[None, :]).astype(jnp.bfloat16)
    right_b, basis_out = (
        lax.all_gather(right_piece, "row", axis=0, tiled=True),
        lax.all_gather(basis_piece, "row", axis=0, tiled=True),
    )
    feedback = lax.dot_general(
        ortho, right_b, (((1,), (1,)), ((), ())), preferred_element_type=jnp.float32
    )
    momentum_out = (buffer.astype(jnp.float32) - ERR * feedback).astype(jnp.bfloat16)
    direction = lax.dot_general(
        ortho, basis_out, (((1,), (1,)), ((), ())), preferred_element_type=jnp.float32
    )
    update = (math.sqrt(D / RANK) * direction).astype(jnp.bfloat16)
    return (momentum_out, basis_out, update)


def solution(mesh):
    placed = (P("row", "col"), P("row", "col"), P("col", None), P(), P())
    return jax.shard_map(
        on_device,
        mesh=mesh,
        in_specs=placed,
        out_specs=(P("row", "col"), P("col", None), P("row", "col")),
        check_vma=False,
    )
```

profile of v0, /device:TPU:0, one launch (start us, length us, event | category | flops | bytes accessed | tf_op | source)
XLA Modules:
  0.0 635.3 jit_solution(6499399184790909212)
XLA Ops:
  7.2 1.2 dynamic_slice.7
  9.1 1.2 dynamic_slice.6
  11.0 15.4 %and_select_fusion = bf16[2176,3840]{1,0:T(8,128)(2,1)S(1)} fusion(bf16[2176,3840]{1,0:T(8,128)(2,1)} %param.6, bf16[2176,3840]{1,0:T(8,128)(2,1)} %param.5, pred[3840]{0:T(1024)(128)(4,1)S(1)} %iota_compare_fusion.4, pred[2176]{0:T(1024)(128)(4,1)S(1)} %iota_compare_fusion.5), kind=kLoop, calls=%fused_computation.5 | loop fusion | flops 50135040 | bytes 50141056 | tf_op jit(solution)/shard_map/jit(_where)/select_n | solution.py:31
  26.5 6.1 copy-done
  32.6 11.3 %fusion = f32[2176,512]{1,0:T(8,128)} fusion(bf16[2176,3840]{1,0:T(8,128)(2,1)S(1)} %and_select_fusion, bf16[3840,512]{1,0:T(8,128)(2,1)S(1)} %copy-done.1, pred[3840]{0:T(1024)(128)(4,1)S(1)} %iota_compare_fusion.4), kind=kOutput, calls=%fused_computation.7 | convolution fusion | flops 8558346240 | bytes 25104128 | tf_op jit(solution)/shard_map/dot_general | solution.py:33
  44.0 165.8 %all-reduce.4.cloned.1.call-done = f32[2176,512]{1,0:T(8,128)} async-done(((f32[2176,512]{1,0:T(8,128)}), f32[2176,512]{1,0:T(8,128)}) %all-reduce.4.cloned.1.call-update) | async-done | bytes 4456464 | tf_op jit(solution)/shard_map/psum | solution.py:34
  209.9 12.1 %fusion.45 = f32[512,512]{0,1:T(8,128)} fusion(f32[2176,512]{1,0:T(8,128)} %all-reduce.4.cloned.1.call-done), kind=kOutput, calls=%fused_computation.91 | convolution fusion | flops 6845104128 | bytes 5505024 | tf_op jit(solution)/shard_map/dot_general | solution.py:35
  222.0 0.5 reduce-scatter.2.cloned.1.call-start
  222.5 0.8 iota_compare_fusion
  223.4 34.0 %all-reduce.6.cloned.1.call-done = f32[512,512]{0,1:T(8,128)} async-done(((f32[512,512]{0,1:T(8,128)}), f32[512,512]{0,1:T(8,128)}) %all-reduce.6.cloned.1.call-update) | async-done | bytes 1048592 | tf_op jit(solution)/shard_map/psum | solution.py:36
  257.4 1.6 copy.9
  259.0 1.4 fusion.11
  260.5 11.7 %cholesky.104 = f32[128,128]{1,0:T(8,128)S(1)} custom-call(f32[128,128]{1,0:T(8,128)S(1)} %cholesky.266), custom_call_target="Cholesky" | custom-call | tf_op jit(solution)/shard_map/jit(cholesky)/cholesky | solution.py:19
  272.2 9.8 %custom-call.31 = f32[1,128,128]{1,2,0:T(8,128)S(1)} custom-call(f32[1,128,128]{2,1,0:T(8,128)S(1)} %get-tuple-element.32), custom_call_target="InvertDiagBlocksLowerTriangular" | custom-call | tf_op jit(solution)/shard_map/jit(cholesky)/cholesky | solution.py:19
  282.8 11.7 %cholesky.217 = f32[128,128]{1,0:T(8,128)S(1)} custom-call(f32[128,128]{1,0:T(8,128)S(1)} %cholesky.270), custom_call_target="Cholesky" | custom-call | tf_op jit(solution)/shard_map/jit(cholesky)/cholesky | solution.py:19
  294.6 9.9 %custom-call.32 = f32[1,128,128]{1,2,0:T(8,128)S(1)} custom-call(f32[1,128,128]{2,1,0:T(8,128)S(1)} %get-tuple-element.29), custom_call_target="InvertDiagBlocksLowerTriangular" | custom-call | tf_op jit(solution)/shard_map/jit(cholesky)/cholesky | solution.py:19
  305.2 11.7 %cholesky.238 = f32[128,128]{1,0:T(8,128)S(1)} custom-call(f32[128,128]{1,0:T(8,128)S(1)} %cholesky.275), custom_call_target="Cholesky" | custom-call | tf_op jit(solution)/shard_map/jit(cholesky)/cholesky | solution.py:19
  317.0 0.6 compare_reduce_fusion.1
  317.6 9.8 %custom-call.33 = f32[1,128,128]{1,2,0:T(8,128)S(1)} custom-call(f32[1,128,128]{2,1,0:T(8,128)S(1)} %get-tuple-element.26), custom_call_target="InvertDiagBlocksLowerTriangular" | custom-call | tf_op jit(solution)/shard_map/jit(cholesky)/cholesky | solution.py:19
  328.0 11.7 %cholesky.255 = f32[128,128]{1,0:T(8,128)S(1)} custom-call(f32[128,128]{1,0:T(8,128)S(1)} %convolution_subtract_fusion.5), custom_call_target="Cholesky" | custom-call | tf_op jit(solution)/shard_map/jit(cholesky)/cholesky | solution.py:19
  339.8 0.7 compare_reduce_fusion
  340.5 0.9 compare_reduce_fusion.2
  344.0 10.1 %while.1 = (s32[]{:T(128)}, f32[512,512]{1,0:T(8,128)S(1)}, s32[4,2]{0,1:T(2,128)S(1)}, f32[4,128,128]{2,1,0:T(8,128)}, s32[]{:T(128)}) while((s32[]{:T(128)}, f32[512,512]{1,0:T(8,128)S(1)}, s32[4,2]{0,1:T(2,128)S(1)}, f32[4,128,128]{2,1,0:T(8,128)}, s32[]{:T(128)}) %tuple.32), condition=%wide.while_cond, body=%wide.while_body.sunk | while | flops 2 | bytes 132205 | solution.py:21
  344.1 0.5 fusion.63
  344.7 1.9 bitcast_dynamic-update-slice_fusion.2
  346.7 0.5 fusion.63
  347.2 1.9 bitcast_dynamic-update-slice_fusion.2
  349.2 0.5 fusion.63
  349.7 1.9 bitcast_dynamic-update-slice_fusion.2
  351.7 0.5 fusion.63
  352.2 1.9 bitcast_dynamic-update-slice_fusion.2
  354.2 40.1 %custom-call.34 = f32[4,128,128]{1,2,0:T(8,128)S(1)} custom-call(f32[4,128,128]{2,1,0:T(8,128)} %get-tuple-element.10), custom_call_target="InvertDiagBlocksLowerTriangular" | custom-call | tf_op jit(solution)/shard_map/jit(_solve_triangular)/triangular_solve | solution.py:21
  394.3 1.1 fusion.22
  395.8 0.4 fusion.34
  396.6 0.4 fusion.32
  397.1 0.6 convolution_subtract_fusion.2
  398.1 9.0 %convolution_convert_fusion = bf16[2176,512]{1,0:T(8,128)(2,1)S(1)} fusion(f32[2176,512]{1,0:T(8,128)} %all-reduce.4.cloned.1.call-done, f32[128,512]{1,0:T(8,128)S(1)} %fusion.31, f32[128,512]{1,0:T(8,128)S(1)} %fusion.32, f32[128,512]{1,0:T(8,128)S(1)} %fusion.34, f32[128,512]{1,0:T(8,128)S(1)} %fusion.22), kind=kOutput, calls=%fused_computation.6 | convolution fusion | flops 6847004672 | bytes 7733248 | tf_op jit(solution)/shard_map/dot_general | solution.py:38
  407.2 15.2 %fusion.46 = f32[3840,512]{1,0:T(8,128)} fusion(bf16[2176,3840]{1,0:T(8,128)(2,1)} %copy-done, bf16[2176,512]{1,0:T(8,128)(2,1)S(1)} %convolution_convert_fusion), kind=kOutput, calls=%fused_computation.92 | convolution fusion | flops 8556380160 | bytes 26804224 | tf_op jit(solution)/shard_map/dot_general | solution.py:40
  422.4 70.1 %reduce-scatter.2.cloned.1.call-done = f32[960,512]{1,0:T(8,128)} async-done(((f32[3840,512]{1,0:T(8,128)}), f32[960,512]{1,0:T(8,128)}) %reduce-scatter.2.cloned.1.call-update) | async-done | bytes 1966096 | tf_op jit(solution)/shard_map/reduce_scatter | solution.py:39
  492.5 1.7 multiply_reduce_fusion
  494.2 39.3 %psum.23 = f32[512]{0:T(512)S(1)} all-reduce(f32[512]{0:T(512)S(1)} %multiply_reduce_fusion), channel_id=1, replica_groups=mesh['row'=4,'col'=8] {'row','col'}, use_global_device_ids=true, to_apply=%region_12.13 | all-reduce | flops 512 | bytes 4096 | tf_op jit(solution)/shard_map/psum | solution.py:47
  533.5 3.8 multiply_convert_fusion.1
  537.4 0.5 all-gather.3.cloned.1.call-update
  537.9 33.3 %all-gather.5.cloned.1.call-done = bf16[3840,512]{1,0:T(8,128)(2,1)} async-done(((bf16[960,512]{1,0:T(8,128)(2,1)}), bf16[3840,512]{1,0:T(8,128)(2,1)}) %all-gather.5.cloned.1.call-update) | async-done | bytes 3932176 | tf_op jit(solution)/shard_map/all_gather | solution.py:53
  571.2 13.9 %multiply_convert_fusion = bf16[2176,3840]{1,0:T(8,128)(2,1)} fusion(bf16[2176,512]{1,0:T(8,128)(2,1)S(1)} %convolution_convert_fusion, bf16[3840,512]{1,0:T(8,128)(2,1)} %all-gather.5.cloned.1.call-done), kind=kOutput, calls=%fused_computation.2 | convolution fusion | flops 8573091840 | bytes 22872064 | tf_op jit(solution)/shard_map/dot_general | solution.py:59
  585.1 20.5 %all-gather.3.cloned.1.call-done = bf16[3840,512]{1,0:T(8,128)(2,1)} async-done(((bf16[960,512]{1,0:T(8,128)(2,1)}), bf16[3840,512]{1,0:T(8,128)(2,1)}) %all-gather.3.cloned.1.call-update) | async-done | bytes 3932176 | tf_op jit(solution)/shard_map/all_gather | solution.py:52
  605.7 18.3 %subtract_convert_fusion = bf16[2176,3840]{1,0:T(8,128)(2,1)} fusion(bf16[2176,3840]{1,0:T(8,128)(2,1)} %copy-done, bf16[2176,512]{1,0:T(8,128)(2,1)S(1)} %convolution_convert_fusion, bf16[3840,512]{1,0:T(8,128)(2,1)} %all-gather.3.cloned.1.call-done), kind=kOutput, calls=%fused_computation.3 | convolution fusion | flops 8589803520 | bytes 39583744 | tf_op jit(solution)/shard_map/dot_general | solution.py:55
  624.0 4.3 copy.30
  (40 shorter events, 4.2 us)
Async XLA Ops:
  7.2 202.7 %all-reduce.4.cloned.1.call-start = ((), (), s32[]{:S(2)}) async-start(), calls=%async_computation.1 | async-start | bytes 8912896 | tf_op jit(solution)/shard_map/psum | solution.py:34
  11.0 21.6 %copy-start.1 = (bf16[3840,512]{1,0:T(8,128)(2,1)S(1)}, bf16[3840,512]{1,0:T(8,128)(2,1)}, u32[]{:S(2)}) copy-start(bf16[3840,512]{1,0:T(8,128)(2,1)} %param.7) | copy-start | bytes 11796484
  26.5 6.1 copy-start
  44.0 213.5 %all-reduce.6.cloned.1.call-start = ((), (), s32[]{:S(2)}) async-start(), calls=%async_computation.2 | async-start | bytes 2097152 | tf_op jit(solution)/shard_map/psum | solution.py:36
  222.0 270.5 %reduce-scatter.2.cloned.1.call-start = ((), (), s32[]{:S(2)}) async-start(), calls=%async_computation.3 | async-start | bytes 9830400 | tf_op jit(solution)/shard_map/reduce_scatter | solution.py:39
  422.4 148.9 %all-gather.5.cloned.1.call-start = ((), (), s32[]{:S(2)}) async-start(), calls=%async_computation.5 | async-start | bytes 4915200 | tf_op jit(solution)/shard_map/all_gather | solution.py:53
  537.3 68.3 %all-gather.3.cloned.1.call-start = ((), (), s32[]{:S(2)}) async-start(), calls=%async_computation.4 | async-start | bytes 4915200 | tf_op jit(solution)/shard_map/all_gather | solution.py:52
Sparse Core Ops, SparseCore 0:
  44.1 165.7 all-reduce.3
  222.1 35.2 all-reduce.5
  422.5 69.9 reduce-scatter.1
  537.5 33.7 all-gather.4
  572.7 32.9 all-gather.2
where the time goes:
time: 643 us; the launch traced here: 635 us
  waiting for transfers between devices  324 us (50%)
  other arithmetic  142 us (22%)
  matrix products  85.5 us (13%)
  blocking collectives  39.3 us (6%)
  local copies, waits for them, and re-layouts  24.7 us (4%)
  between operations  18.3 us (3%)
    psum x1, waiting for transfers between devices, on_device(): left_part = lax.psum(partial_left, 'col')  166 us
    another operation x14, other arithmetic, tri_inverse(): lower_factor = jnp.linalg.cholesky(gram_matrix)  78.8 us
    reduce_scatter x1, waiting for transfers between devices, on_device(): lax.psum_scatter(lax.dot_general(buffer, ortho, (((0,), (0,)), ((), ())),...  70.1 us
    another operation x3, other arithmetic, tri_inverse(): return jax.scipy.linalg.solve_triangular(lower_factor, ident, lower=True)  40.3 us
    psum x1, blocking collectives, on_device(): squares = lax.psum(jnp.sum(right_part * right_part, axis=0), ('row', 'col'))  39.3 us
    psum x1, waiting for transfers between devices, on_device(): gram_matrix = lax.psum(gram_local, 'row')  34 us
    all_gather x1, waiting for transfers between devices, on_device(): lax.all_gather(basis_piece, 'row', axis=0, tiled=True)  33.3 us
    all_gather x1, waiting for transfers between devices, on_device(): lax.all_gather(right_piece, 'row', axis=0, tiled=True)  20.5 us
  transfers between devices with their start and end apart: 5, of which 5 were waited for; matrix products, arithmetic and copies ran while one was open for 2% of the time, Pallas kernels for 0%

commit v1 on v0

v1 whole, which is shorter than its diff:
```python
import math

import jax
import jax.numpy as jnp
from jax import lax
from jax.experimental import pallas as pl
from jax.experimental.pallas import tpu as pltpu
from jax.sharding import PartitionSpec as P

D = 8192
FF = 28672
RANK = 512
BLOCK = 128


EPS = 1e-06
ERR = 0.05


HIGHEST = lax.Precision.HIGHEST
TILE = 128
SUB = 8


def matmul(left, right, contract):
    return lax.dot_general(
        left, right, (contract, ((), ())), precision=HIGHEST, preferred_element_type=jnp.float32
    )


def tile_inverse(rows, size):
    groups = size // SUB
    sub = lax.broadcasted_iota(jnp.int32, (SUB, size), 0)
    lane = lax.broadcasted_iota(jnp.int32, (SUB, size), 1)
    inv = [jnp.where(lane == sub + SUB * g, 1.0, 0.0) for g in range(groups)]
    for j in range(size):
        g0, s = divmod(j, SUB)
        row = rows[g0][s : s + 1, :]
        pivot = jnp.broadcast_to(row[:, j : j + 1], (1, size))
        scale = lax.rsqrt(pivot)
        scale = scale * (1.5 - 0.5 * pivot * scale * scale)
        low_row = row * scale
        inv_row = inv[g0][s : s + 1, :] * scale
        low_times = low_row * scale
        inv_times = inv_row * scale
        for g in range(g0, groups):
            factor = jnp.broadcast_to(rows[g][:, j : j + 1], (SUB, size))
            if g == g0:
                factor = jnp.where(sub > s, factor, 0.0)
                inv[g] = jnp.where(sub == s, inv_row, inv[g] - factor * inv_times)
            else:
                inv[g] = inv[g] - factor * inv_times
            rows[g] = rows[g] - factor * low_times
    return jnp.concatenate(inv, axis=0)


def inverse_kernel(gram_ref, out_ref, work_ref):
    rank = gram_ref.shape[0]
    work_ref[...] = gram_ref[...]
    row_id = lax.broadcasted_iota(jnp.int32, (rank, rank), 0)
    col_id = lax.broadcasted_iota(jnp.int32, (rank, rank), 1)
    out_ref[...] = jnp.where(row_id == col_id, 1.0, 0.0)

    def step(k, carry):
        base = pl.multiple_of(k * TILE, TILE)
        here = pl.ds(base, TILE)
        rows = [
            work_ref[pl.ds(pl.multiple_of(base + SUB * g, SUB), SUB), here]
            for g in range(TILE // SUB)
        ]
        tile_inv = tile_inverse(rows, TILE)
        panel = matmul(work_ref[:, here], tile_inv, ((1,), (1,)))
        below = lax.broadcasted_iota(jnp.int32, (rank, TILE), 0) >= base + TILE
        panel = jnp.where(below, panel, 0.0)
        solved = matmul(tile_inv, out_ref[here, :], ((1,), (0,)))
        work_ref[...] = work_ref[...] - matmul(panel, panel, ((1,), (1,)))
        out_ref[...] = out_ref[...] - matmul(panel, solved, ((1,), (0,)))
        out_ref[here, :] = solved
        return carry

    lax.fori_loop(0, rank // TILE, step, 0)


def tri_inverse(gram_matrix):
    return pl.pallas_call(
        inverse_kernel,
        out_shape=jax.ShapeDtypeStruct(gram_matrix.shape, jnp.float32),
        scratch_shapes=[pltpu.VMEM(gram_matrix.shape, jnp.float32)],
    )(gram_matrix)


def on_device(momentum, grad, q_prev, row_counts, col_counts):
    row_slots, col_slots = momentum.shape
    row_live = row_counts[lax.axis_index("row")] * BLOCK
    col_live = col_counts[lax.axis_index("col")] * BLOCK
    row_mask = jnp.arange(row_slots, dtype=jnp.int32) < row_live
    col_mask = jnp.arange(col_slots, dtype=jnp.int32) < col_live
    summed = (momentum.astype(jnp.float32) + grad.astype(jnp.float32)).astype(jnp.bfloat16)
    buffer = jnp.where(row_mask[:, None] & col_mask[None, :], summed, jnp.zeros((), jnp.bfloat16))
    prev_basis = jnp.where(col_mask[:, None], q_prev, jnp.zeros((), jnp.bfloat16))
    partial_left = jnp.dot(buffer, prev_basis, preferred_element_type=jnp.float32)
    left_part = lax.psum_scatter(partial_left, "col", scatter_dimension=0, tiled=True)
    gram_local = jnp.dot(left_part.T, left_part, precision=HIGHEST)
    gram_matrix = lax.psum(gram_local, ("row", "col"))
    inverse = tri_inverse(gram_matrix)
    ortho_piece = jnp.dot(left_part, inverse.T, precision=HIGHEST).astype(jnp.bfloat16)
    ortho = lax.all_gather(ortho_piece, "col", axis=0, tiled=True)
    right_local = lax.dot_general(
        buffer, ortho, (((0,), (0,)), ((), ())), preferred_element_type=jnp.float32
    )
    right_piece = lax.psum_scatter(
        right_local.astype(jnp.bfloat16), "row", scatter_dimension=0, tiled=True
    )
    right_b = lax.all_gather(right_piece, "row", axis=0, tiled=True)
    right_part = right_piece.astype(jnp.float32)
    squares = lax.psum(jnp.sum(right_part * right_part, axis=0), ("row", "col"))
    norm_factor = lax.rsqrt(squares / FF + EPS)
    basis_out = (right_b.astype(jnp.float32) * norm_factor[None, :]).astype(jnp.bfloat16)
    feedback = lax.dot_general(
        ortho, right_b, (((1,), (1,)), ((), ())), preferred_element_type=jnp.float32
    )
    momentum_out = (buffer.astype(jnp.float32) - ERR * feedback).astype(jnp.bfloat16)
    direction = lax.dot_general(
        ortho, basis_out, (((1,), (1,)), ((), ())), preferred_element_type=jnp.float32
    )
    update = (math.sqrt(D / RANK) * direction).astype(jnp.bfloat16)
    return (momentum_out, basis_out, update)


def solution(mesh):
    placed = (P("row", "col"), P("row", "col"), P("col", None), P(), P())
    return jax.shard_map(
        on_device,
        mesh=mesh,
        in_specs=placed,
        out_specs=(P("row", "col"), P("col", None), P("row", "col")),
        check_vma=False,
    )
```

time: 643 us -> 527 us (0.82); the launches traced: 635 us -> 527 us
  other arithmetic: 142 us -> 19.8 us
  Pallas kernels: 0 us -> 59.5 us
  matrix products: 85.5 us -> 65.9 us
  local copies, waits for them, and re-layouts: 24.7 us -> 8.63 us
    another operation x17 -> x0, other arithmetic: 119 us -> none  [the longest x14 78.8 us: tri_inverse(): lower_factor = jnp.linalg.cholesky(gram_matrix)]
    psum x2 -> x1, waiting for transfers between devices: 200 us -> 132 us  [on_device(): gram_matrix = lax.psum(gram_local, ('row', 'col'))]
    reduce_scatter x1 -> x2, waiting for transfers between devices: 70.1 us -> 136 us  [the longest x1 94.9 us: on_device(): lax.psum_scatter(partial_left, 'col', scatter_dimension=0, tiled=True)]
    pallas_call x0 -> x1, Pallas kernels: none -> 59.5 us  [tri_inverse(): pl.pallas_call(inverse_kernel, out_shape=jax.ShapeDtypeStruct(gram_matrix...]
    dot_general x2, matrix products: 21.1 us -> 7.24 us  [the longest x1 4.03 us: on_device(): gram_local = jnp.dot(left_part.T, left_part, precision=HIGHEST)]
    another operation x17 -> x0, local copies, waits for them, and re-layouts: 10.3 us -> none
  transfers between devices with their start and end apart: 5 -> 5, of which waited for: 5 -> 4; matrix products, arithmetic and copies ran while one was open for 2% -> 0% of each run, Pallas kernels for 0% -> 0%
where the time goes in v1:
time: 527 us
  waiting for transfers between devices  318 us (60%)
  matrix products  65.9 us (13%)
  Pallas kernels  59.5 us (11%)
  blocking collectives  39.7 us (8%)
  other arithmetic  19.8 us (4%)
  between operations  15.2 us (3%)
  local copies, waits for them, and re-layouts  8.63 us (2%)
    psum x1, waiting for transfers between devices, on_device(): gram_matrix = lax.psum(gram_local, ('row', 'col'))  132 us
    reduce_scatter x1, waiting for transfers between devices, on_device(): lax.psum_scatter(partial_left, 'col', scatter_dimension=0, tiled=True)  94.9 us
    pallas_call x1, Pallas kernels, tri_inverse(): pl.pallas_call(inverse_kernel, out_shape=jax.ShapeDtypeStruct(gram_matrix...  59.5 us
    all_gather x1, waiting for transfers between devices, on_device(): ortho = lax.all_gather(ortho_piece, 'col', axis=0, tiled=True)  49.4 us
    reduce_scatter x1, waiting for transfers between devices, on_device(): lax.psum_scatter(right_local.astype(jnp.bfloat16), 'row', scatter_dimensi...  41.3 us
    psum x1, blocking collectives, on_device(): squares = lax.psum(jnp.sum(right_part * right_part, axis=0), ('row', 'col'))  39.7 us
    dot_general x1, matrix products, on_device(): lax.dot_general(ortho, right_b, (((1,), (1,)), ((), ())), preferred_eleme...  18.4 us
    dot_general x1, matrix products, on_device(): lax.dot_general(buffer, ortho, (((0,), (0,)), ((), ())), preferred_elemen...  17.2 us
  transfers between devices with their start and end apart: 5, of which 4 were waited for; matrix products, arithmetic and copies ran while one was open for 0% of the time, Pallas kernels for 0%

profile of v1, /device:TPU:0, one launch (start us, length us, event | category | flops | bytes accessed | tf_op | source)
XLA Modules:
  0.0 526.8 jit_solution(18243613012445500195)
XLA Ops:
  7.2 0.0 reduce-scatter.3.cloned.1.call-start
  7.2 1.2 dynamic_slice.7
  9.1 1.2 dynamic_slice.6
  11.0 0.0 copy-start.2
  11.0 15.4 %and_select_fusion = bf16[2176,3840]{1,0:T(8,128)(2,1)S(1)} fusion(bf16[2176,3840]{1,0:T(8,128)(2,1)} %param.6, bf16[2176,3840]{1,0:T(8,128)(2,1)} %param.5, pred[3840]{0:T(1024)(128)(4,1)S(1)} %iota_compare_fusion, pred[2176]{0:T(1024)(128)(4,1)S(1)} %iota_compare_fusion.1), kind=kLoop, calls=%fused_computation.3 | loop fusion | flops 50135040 | bytes 50141056 | tf_op jit(solution)/shard_map/jit(_where)/select_n | solution.py:99
  26.5 0.0 copy-start
  26.5 6.1 %copy-done = bf16[2176,3840]{1,0:T(8,128)(2,1)} copy-done((bf16[2176,3840]{1,0:T(8,128)(2,1)}, bf16[2176,3840]{1,0:T(8,128)(2,1)S(1)}, u32[]{:S(2)}) %copy-start) | copy-done | bytes 16711704
  32.6 0.0 copy-done.2
  32.6 11.3 %fusion = f32[2176,512]{1,0:T(8,128)} fusion(bf16[2176,3840]{1,0:T(8,128)(2,1)S(1)} %and_select_fusion, bf16[3840,512]{1,0:T(8,128)(2,1)S(1)} %copy-done.2, pred[3840]{0:T(1024)(128)(4,1)S(1)} %iota_compare_fusion), kind=kOutput, calls=%fused_computation.6 | convolution fusion | flops 8558346240 | bytes 25104128 | tf_op jit(solution)/shard_map/dot_general | solution.py:101
  43.9 0.0 reduce-scatter.3.cloned.1.call-update
  44.0 0.0 all-reduce.2.cloned.1.call-start
  44.0 94.9 %reduce-scatter.3.cloned.1.call-done = f32[272,512]{1,0:T(8,128)} async-done(((f32[2176,512]{1,0:T(8,128)}), f32[272,512]{1,0:T(8,128)}) %reduce-scatter.3.cloned.1.call-update) | async-done | bytes 557072 | tf_op jit(solution)/shard_map/reduce_scatter | solution.py:102
  138.9 4.0 fusion.5
  143.0 0.0 all-reduce.2.cloned.1.call-update
  143.0 0.2 all-gather.3.cloned.1.call-start
  143.2 131.8 %all-reduce.2.cloned.1.call-done.gram_ref = f32[512,512]{1,0:T(8,128)} async-done(((f32[512,512]{1,0:T(8,128)}), f32[512,512]{1,0:T(8,128)}) %all-reduce.2.cloned.1.call-update) | async-done | bytes 1048592 | tf_op jit(solution)/shard_map/psum | solution.py:104
  275.0 59.5 %shard_map.76 = f32[512,512]{1,0:T(8,128)} custom-call(f32[512,512]{1,0:T(8,128)} %all-reduce.2.cloned.1.call-done.gram_ref), custom_call_target="tpu_custom_call" | custom-call | tf_op jit(solution)/shard_map/pallas_call | solution.py:85
  334.5 3.2 convolution_convert_fusion.1
  337.7 0.0 all-gather.3.cloned.1.call-update
  337.8 0.0 reduce-scatter.5.cloned.1.call-start
  337.8 49.4 %all-gather.3.cloned.1.call-done = bf16[2176,512]{1,0:T(8,128)(2,1)} async-done(((bf16[272,512]{1,0:T(8,128)(2,1)}), bf16[2176,512]{1,0:T(8,128)(2,1)}) %all-gather.3.cloned.1.call-update) | async-done | bytes 2228240 | tf_op jit(solution)/shard_map/all_gather | solution.py:107
  387.2 0.0 copy-start.3
  387.2 17.2 %convolution_convert_fusion = bf16[3840,512]{1,0:T(8,128)(2,1)} fusion(bf16[2176,3840]{1,0:T(8,128)(2,1)} %copy-done, bf16[2176,512]{1,0:T(8,128)(2,1)} %all-gather.3.cloned.1.call-done), kind=kOutput, calls=%fused_computation.5 | convolution fusion | flops 8558346240 | bytes 22872064 | tf_op jit(solution)/shard_map/dot_general | solution.py:108
  404.4 0.0 reduce-scatter.5.cloned.1.call-update
  404.5 0.3 all-gather.5.cloned.1.call-start
  404.7 41.3 %reduce-scatter.5.cloned.1.call-done = bf16[960,512]{1,0:T(8,128)(2,1)} async-done(((bf16[3840,512]{1,0:T(8,128)(2,1)}), bf16[960,512]{1,0:T(8,128)(2,1)}) %reduce-scatter.5.cloned.1.call-update) | async-done | bytes 983056 | tf_op jit(solution)/shard_map/reduce_scatter | solution.py:111
  446.1 0.0 all-gather.5.cloned.1.call-update
  446.1 1.5 multiply_reduce_fusion
  447.6 39.7 %psum.15 = f32[512]{0:T(512)S(1)} all-reduce(f32[512]{0:T(512)S(1)} %multiply_reduce_fusion), channel_id=1, replica_groups=mesh['row'=4,'col'=8] {'row','col'}, use_global_device_ids=true, to_apply=%region_4.5 | all-reduce | flops 512 | bytes 4096 | tf_op jit(solution)/shard_map/psum | solution.py:116
  487.2 0.0 all-gather.5.cloned.1.call-done
  487.2 0.0 copy-done.3
  487.2 18.4 %subtract_convert_fusion = bf16[2176,3840]{1,0:T(8,128)(2,1)} fusion(bf16[2176,3840]{1,0:T(8,128)(2,1)} %copy-done, bf16[2176,512]{1,0:T(8,128)(2,1)S(1)} %copy-done.3, bf16[3840,512]{1,0:T(8,128)(2,1)} %all-gather.5.cloned.1.call-done), kind=kOutput, calls=%fused_computation.1 | convolution fusion | flops 8589803520 | bytes 39583744 | tf_op jit(solution)/shard_map/dot_general | solution.py:119
  505.6 2.9 multiply_convert_fusion.1
  508.5 0.0 copy-start.1
  508.5 11.8 %multiply_convert_fusion = bf16[2176,3840]{1,0:T(8,128)(2,1)} fusion(bf16[2176,512]{1,0:T(8,128)(2,1)S(1)} %copy-done.3, bf16[3840,512]{1,0:T(8,128)(2,1)S(1)} %multiply_convert_fusion.1), kind=kOutput, calls=%fused_computation | convolution fusion | flops 8573091840 | bytes 22872064 | tf_op jit(solution)/shard_map/dot_general | solution.py:123
  520.3 0.0 copy-done.1
  (3 shorter events, 0.0 us)
Async XLA Ops:
  7.2 131.8 %reduce-scatter.3.cloned.1.call-start = ((), (), s32[]{:S(2)}) async-start(), calls=%async_computation.2 | async-start | bytes 5013504 | tf_op jit(solution)/shard_map/reduce_scatter | solution.py:102
  11.0 21.6 %copy-start.2 = (bf16[3840,512]{1,0:T(8,128)(2,1)S(1)}, bf16[3840,512]{1,0:T(8,128)(2,1)}, u32[]{:S(2)}) copy-start(bf16[3840,512]{1,0:T(8,128)(2,1)} %param.7) | copy-start | bytes 11796484
  26.5 6.1 %copy-start = (bf16[2176,3840]{1,0:T(8,128)(2,1)}, bf16[2176,3840]{1,0:T(8,128)(2,1)S(1)}, u32[]{:S(2)}) copy-start(bf16[2176,3840]{1,0:T(8,128)(2,1)S(1)} %and_select_fusion) | copy-start | bytes 50135044
  44.0 231.1 %all-reduce.2.cloned.1.call-start = ((), (), s32[]{:S(2)}) async-start(), calls=%async_computation.3 | async-start | bytes 2097152 | tf_op jit(solution)/shard_map/psum | solution.py:104
  143.0 244.2 %all-gather.3.cloned.1.call-start = ((), (), s32[]{:S(2)}) async-start(), calls=%async_computation.4 | async-start | bytes 2506752 | tf_op jit(solution)/shard_map/all_gather | solution.py:107
  337.8 108.3 %reduce-scatter.5.cloned.1.call-start = ((), (), s32[]{:S(2)}) async-start(), calls=%async_computation.5 | async-start | bytes 4915200 | tf_op jit(solution)/shard_map/reduce_scatter | solution.py:111
  387.2 100.0 %copy-start.3 = (bf16[2176,512]{1,0:T(8,128)(2,1)S(1)}, bf16[2176,512]{1,0:T(8,128)(2,1)}, u32[]{:S(2)}) copy-start(bf16[2176,512]{1,0:T(8,128)(2,1)} %all-gather.3.cloned.1.call-done) | copy-start | bytes 6684676
  404.5 82.8 %all-gather.5.cloned.1.call-start = ((), (), s32[]{:S(2)}) async-start(), calls=%async_computation.6 | async-start | bytes 4915200 | tf_op jit(solution)/shard_map/all_gather | solution.py:114
  508.5 11.8 %copy-start.1 = (bf16[3840,512]{1,0:T(8,128)(2,1)}, bf16[3840,512]{1,0:T(8,128)(2,1)S(1)}, u32[]{:S(2)}) copy-start(bf16[3840,512]{1,0:T(8,128)(2,1)S(1)} %multiply_convert_fusion.1) | copy-start | bytes 11796484
Sparse Core Ops, SparseCore 0:
  44.1 94.8 reduce-scatter.2
  144.7 130.2 all-reduce.1
  337.9 49.3 all-gather.2
  404.6 41.4 reduce-scatter.4
  447.5 33.2 all-gather.4
